TPU v7x, 32 devices: a whole 2x2x4 slice. The times are simulated.
32 devices in a mesh: dp: 8 (over y, x, core), tensor: 4 (over z).
Axes of the slice: x: 2, y: 2, z: 4, core: 2. Of those that a mesh axis runs over, the one named last changes fastest.
Arguments:
- grad_out: bfloat16 [2048, 4096], P('dp'), may hold values from -6 to 6
- down_weight: bfloat16 [14336, 4096], P('tensor'), may hold values from -0.046875 to 0.046875
- gate_pre: bfloat16 [2048, 14336], P('dp', 'tensor'), may hold values from -8 to 8
- up_pre: bfloat16 [2048, 14336], P('dp', 'tensor'), may hold values from -6 to 6
Outputs:
- factor: float32 [14336, 14336], P('dp', 'tensor')
- grad_up: bfloat16 [2048, 14336], P('dp', 'tensor')
All inputs are finite; a program needn't handle non-finite values.
Results may differ from a plain program's by a relative error of at most 0.0046.
Values may be sent and summed in bfloat16 or wider, within the bound.
A program may use at most 128 MiB of HBM per device.

v0:
```python
import jax
import jax.numpy as jnp
from jax import lax
from jax.sharding import PartitionSpec as P


def local(grad_out, down_weight, gate_pre, up_pre):
    hidden_grad = lax.dot_general(
        grad_out, down_weight, (((1,), (1,)), ((), ())), preferred_element_type=jnp.float32
    )
    gate_value = gate_pre.astype(jnp.float32)
    sigmoid_gate = jax.nn.sigmoid(gate_value)
    silu_slope = sigmoid_gate * (1.0 + gate_value * (1.0 - sigmoid_gate))
    grad_gate = (hidden_grad * up_pre.astype(jnp.float32) * silu_slope).astype(jnp.bfloat16)
    grad_up = (hidden_grad * gate_value * sigmoid_gate).astype(jnp.bfloat16)
    replicas = lax.axis_size("dp")
    token_total = grad_gate.shape[0] * replicas
    all_columns_grad = lax.all_gather(grad_gate, "tensor", axis=1, tiled=True)
    row_block = lax.all_to_all(all_columns_grad, "dp", split_axis=1, concat_axis=0, tiled=True)
    factor_tile = lax.dot_general(
        row_block,
        lax.all_gather(grad_gate, "dp", axis=0, tiled=True),
        (((0,), (0,)), ((), ())),
        preferred_element_type=jnp.float32,
    )
    factor = factor_tile / jnp.float32(token_total)
    return (factor, grad_up)


def solution(mesh):
    placed = (P("dp", None), P("tensor", None), P("dp", "tensor"), P("dp", "tensor"))
    return jax.shard_map(
        local,
        mesh=mesh,
        in_specs=placed,
        out_specs=(P("dp", "tensor"), P("dp", "tensor")),
        check_vma=False,
    )
```

profile of v0, /device:TPU:0, one launch (start us, length us, event | category | flops | bytes accessed | tf_op | source)
XLA Modules:
  0.0 351.9 jit_solution(13841127326262000508)
XLA Ops:
  7.2 0.0 copy-start
  7.2 0.0 all-gather.3.cloned.1.call-start
  7.2 1.5 copy-done
  8.8 16.8 %fusion.8 = (bf16[256,3584]{1,0:T(8,128)(2,1)}, bf16[256,3584]{1,0:T(8,128)(2,1)}) fusion(bf16[256,3584]{1,0:T(8,128)(2,1)} %param.6, bf16[256,3584]{1,0:T(8,128)(2,1)} %param.7, bf16[256,4096]{1,0:T(8,128)(2,1)S(1)} %copy-done, bf16[3584,4096]{1,0:T(8,128)(2,1)} %param.5), kind=kOutput, calls=%fused_computation.13 | convolution fusion | flops 7529955328 | bytes 38797312 | tf_op jit(solution)/shard_map/dot_general | solution.py:8
  25.6 0.0 all-gather.3.cloned.1.call-update
  25.6 0.0 all-gather.5.cloned.1.call-start
  25.7 0.7 all-gather.5.cloned.1.call-update
  26.4 134.6 %all-gather.3.cloned.1.call-done = bf16[256,14336]{1,0:T(8,128)(2,1)} async-done(((bf16[256,3584]{1,0:T(8,128)(2,1)}), bf16[256,14336]{1,0:T(8,128)(2,1)}) %all-gather.3.cloned.1.call-update) | async-done | bytes 7340048 | tf_op jit(solution)/shard_map/all_gather | solution.py:18
  161.0 3.6 %copy.9 = bf16[32,8,8,1792]{3,2,0,1:T(8,128)(2,1)S(1)} copy(bf16[32,8,8,1792]{3,2,1,0:T(8,128)(2,1)} %bitcast.12) | data formatting | bytes 14680064 | tf_op jit(solution)/shard_map/all_to_all | solution.py:19
  164.5 135.2 %all_to_all.19 = bf16[256,8,1792]{2,0,1:T(8,128)(2,1)} all-to-all(bf16[256,8,1792]{2,0,1:T(8,128)(2,1)S(1)} %bitcast.11), channel_id=1, replica_groups=mesh['dp'=8,'tensor'=4] {'dp'}, dimensions={1} | all-to-all | bytes 14680064 | tf_op jit(solution)/shard_map/all_to_all | solution.py:19
  299.8 11.4 %all-gather.5.cloned.1.call-done = bf16[2048,3584]{1,0:T(8,128)(2,1)} async-done(((bf16[256,3584]{1,0:T(8,128)(2,1)}), bf16[2048,3584]{1,0:T(8,128)(2,1)}) %all-gather.5.cloned.1.call-update) | async-done | bytes 14680080 | tf_op jit(solution)/shard_map/all_gather | solution.py:22
  311.2 0.0 copy-start.1
  311.2 33.9 %convolution_multiply_fusion = f32[1792,3584]{1,0:T(8,128)} fusion(bf16[2048,1792]{1,0:T(8,128)(2,1)} %bitcast.13, bf16[2048,3584]{1,0:T(8,128)(2,1)} %all-gather.5.cloned.1.call-done), kind=kOutput, calls=%fused_computation | convolution fusion | flops 26313097216 | bytes 47710208 | tf_op jit(solution)/shard_map/dot_general | solution.py:20
  345.1 0.0 copy-done.1
Async XLA Ops:
  7.2 1.6 copy-start
  7.2 153.8 %all-gather.3.cloned.1.call-start = ((), (), s32[]{:S(2)}) async-start(), calls=%async_computation.1 | async-start | bytes 9175040 | tf_op jit(solution)/shard_map/all_gather | solution.py:18
  25.6 285.6 %all-gather.5.cloned.1.call-start = ((), (), s32[]{:S(2)}) async-start(), calls=%async_computation.2 | async-start | bytes 16515072 | tf_op jit(solution)/shard_map/all_gather | solution.py:22
  311.2 33.9 %copy-start.1 = (bf16[256,4096]{1,0:T(8,128)(2,1)S(1)}, bf16[256,4096]{1,0:T(8,128)(2,1)}, u32[]{:S(2)}) copy-start(bf16[256,4096]{1,0:T(8,128)(2,1)} %param.4) | copy-start | bytes 6291460
Sparse Core Ops, SparseCore 0:
  25.7 135.1 all-gather.2
  163.4 147.7 all-gather.4
where the time goes:
time: 352 us
  waiting for transfers between devices  147 us (42%)
  blocking collectives  135 us (38%)
  matrix products  50.7 us (14%)
  between operations  14.1 us (4%)
  local copies, waits for them, and re-layouts  5.11 us (1%)
    all_to_all x1, blocking collectives, local(): lax.all_to_all(all_columns_grad, 'dp', split_axis=1, concat_axis=0, tiled...  135 us
    all_gather x1, waiting for transfers between devices, local(): all_columns_grad = lax.all_gather(grad_gate, 'tensor', axis=1, tiled=True)  135 us
    dot_general x1, matrix products, local(): lax.dot_general(row_block, lax.all_gather(grad_gate, 'dp', axis=0, tiled=...  33.9 us
    dot_general x1, matrix products, local(): lax.dot_general(grad_out, down_weight, (((1,), (1,)), ((), ())), preferre...  16.8 us
    all_gather x1, waiting for transfers between devices, local(): lax.all_gather(grad_gate, 'dp', axis=0, tiled=True)  11.4 us
  transfers between devices with their start and end apart: 2, of which 2 were waited for; matrix products, arithmetic and copies ran while one was open for 1% of the time, Pallas kernels for 0%

commit v1 on v0

--- a/solution.py
+++ b/solution.py
@@ -2,6 +2,17 @@
 import jax.numpy as jnp
 from jax import lax
 from jax.sharding import PartitionSpec as P
+
+
+def gather_by_hops(shard, axis, d):
+    size = lax.axis_size(axis)
+    right = [(i, (i + 1) % size) for i in range(size)]
+    pieces = [shard]
+    for far in range(1, size):
+        pieces = [lax.ppermute(pieces[0], axis, right), *pieces]
+    result = jnp.concatenate(pieces, axis=d)
+    turn = (lax.axis_index(axis) + 1) * pieces[-1].shape[d]
+    return jnp.roll(result, turn, axis=d)
 
 
 def local(grad_out, down_weight, gate_pre, up_pre):
@@ -15,7 +26,7 @@
     grad_up = (hidden_grad * gate_value * sigmoid_gate).astype(jnp.bfloat16)
     replicas = lax.axis_size("dp")
     token_total = grad_gate.shape[0] * replicas
-    all_columns_grad = lax.all_gather(grad_gate, "tensor", axis=1, tiled=True)
+    all_columns_grad = gather_by_hops(grad_gate, "tensor", 1)
     row_block = lax.all_to_all(all_columns_grad, "dp", split_axis=1, concat_axis=0, tiled=True)
     factor_tile = lax.dot_general(
         row_block,

time: 352 us -> 334 us (0.949)
  blocking collectives: 135 us -> 88.3 us
  local copies, waits for them, and re-layouts: 5.11 us -> 48.7 us
  waiting for transfers between devices: 147 us -> 128 us
    all_gather x1 -> x0, waiting for transfers between devices: 135 us -> none  [local(): all_columns_grad = lax.all_gather(grad_gate, 'tensor', axis=1, tiled=True)]
    ppermute x0 -> x3, waiting for transfers between devices: none -> 128 us  [gather_by_hops(): pieces = [lax.ppermute(pieces[0], axis, right), *pieces]]
    all_to_all x1, blocking collectives: 135 us -> 88.3 us  [local(): lax.all_to_all(all_columns_grad, 'dp', split_axis=1, concat_axis=0, tiled...]
    dynamic_slice x0 -> x2, local copies, waits for them, and re-layouts: none -> 19.1 us  [gather_by_hops(): return jnp.roll(result, turn, axis=d)]
    unnamed x4 -> x17, local copies, waits for them, and re-layouts: 1.55 us -> 18.2 us
    all_gather x1, waiting for transfers between devices: 11.4 us -> 0.01 us  [local(): lax.all_gather(grad_gate, 'dp', axis=0, tiled=True)]
    all_to_all x1, local copies, waits for them, and re-layouts: 3.56 us -> 10.1 us  [local(): lax.all_to_all(all_columns_grad, 'dp', split_axis=1, concat_axis=0, tiled...]
  transfers between devices with their start and end apart: 2 -> 4, of which waited for: 2 -> 3; matrix products, arithmetic and copies ran while one was open for 1% -> 14% of each run, Pallas kernels for 0% -> 0%
where the time goes in v1:
time: 334 us; the launch traced here: 333 us
  waiting for transfers between devices  128 us (38%)
  blocking collectives  88.3 us (26%)
  matrix products  50.7 us (15%)
  local copies, waits for them, and re-layouts  48.7 us (15%)
  between operations  14 us (4%)
    ppermute x3, waiting for transfers between devices, gather_by_hops(): pieces = [lax.ppermute(pieces[0], axis, right), *pieces]  128 us
    all_to_all x1, blocking collectives, local(): lax.all_to_all(all_columns_grad, 'dp', split_axis=1, concat_axis=0, tiled...  88.3 us
    dot_general x1, matrix products, local(): lax.dot_general(row_block, lax.all_gather(grad_gate, 'dp', axis=0, tiled=...  33.9 us
    dynamic_slice x2, local copies, waits for them, and re-layouts, gather_by_hops(): return jnp.roll(result, turn, axis=d)  19.1 us
    unnamed x17, local copies, waits for them, and re-layouts  18.2 us
    dot_general x1, matrix products, local(): lax.dot_general(grad_out, down_weight, (((1,), (1,)), ((), ())), preferre...  16.9 us
    all_to_all x1, local copies, waits for them, and re-layouts, local(): lax.all_to_all(all_columns_grad, 'dp', split_axis=1, concat_axis=0, tiled...  10.1 us
  transfers between devices with their start and end apart: 4, of which 3 were waited for; matrix products, arithmetic and copies ran while one was open for 14% of the time, Pallas kernels for 0%

profile of v1, /device:TPU:0, one launch (start us, length us, event | category | flops | bytes accessed | tf_op | source)
XLA Modules:
  0.0 332.7 jit_solution(17324642808825691218)
XLA Ops:
  7.2 0.0 copy-start
  7.2 0.0 all-gather.2.cloned.1.call-start
  7.2 1.5 copy-done
  8.8 16.9 %fusion.8 = (bf16[256,3584]{1,0:T(8,128)(2,1)}, bf16[256,3584]{1,0:T(8,128)(2,1)}) fusion(bf16[256,3584]{1,0:T(8,128)(2,1)} %param.6, bf16[256,3584]{1,0:T(8,128)(2,1)} %param.7, bf16[256,4096]{1,0:T(8,128)(2,1)S(1)} %copy-done, bf16[3584,4096]{1,0:T(8,128)(2,1)} %param.5), kind=kOutput, calls=%fused_computation.12 | convolution fusion | flops 7529955328 | bytes 38797312 | tf_op jit(solution)/shard_map/dot_general | solution.py:19
  25.6 0.0 copy-start.2
  25.6 0.0 all-gather.2.cloned.1.call-update
  25.7 3.1 collective-permute-start
  28.8 42.2 %collective-permute-done = bf16[256,3584]{1,0:T(8,128)(2,1)S(1)} collective-permute-done((bf16[256,3584]{1,0:T(8,128)(2,1)}, bf16[256,3584]{1,0:T(8,128)(2,1)S(1)}, u32[]{:S(2)}, u32[]{:S(2)}) %collective-permute-start) | collective-permute-done | bytes 1835040 | tf_op jit(solution)/shard_map/ppermute | solution.py:12
  71.0 0.0 copy-start.3
  71.0 1.2 copy-done.3
  72.3 0.0 collective-permute-start.1
  72.3 43.1 %collective-permute-done.1 = bf16[256,3584]{1,0:T(8,128)(2,1)} collective-permute-done((bf16[256,3584]{1,0:T(8,128)(2,1)S(1)}, bf16[256,3584]{1,0:T(8,128)(2,1)}, u32[]{:S(2)}, u32[]{:S(2)}) %collective-permute-start.1) | collective-permute-done | bytes 1835040 | tf_op jit(solution)/shard_map/ppermute | solution.py:12
  115.3 0.0 collective-permute-start.2
  115.3 0.0 copy-start.4
  115.3 42.4 %collective-permute-done.2 = bf16[256,3584]{1,0:T(8,128)(2,1)} collective-permute-done((bf16[256,3584]{1,0:T(8,128)(2,1)}, bf16[256,3584]{1,0:T(8,128)(2,1)}, u32[]{:S(2)}, u32[]{:S(2)}) %collective-permute-start.2) | collective-permute-done | bytes 1835040 | tf_op jit(solution)/shard_map/ppermute | solution.py:12
  157.8 2.8 constant_dynamic-update-slice_fusion.7
  160.6 2.8 constant_dynamic-update-slice_fusion.6
  163.5 0.0 copy-done.4
  163.5 1.3 constant_dynamic-update-slice_fusion.5
  164.8 0.0 copy-done.2
  164.8 1.3 constant_dynamic-update-slice_fusion.4
  166.2 2.8 constant_dynamic-update-slice_fusion.3
  169.0 2.8 constant_dynamic-update-slice_fusion.2
  171.8 1.3 constant_dynamic-update-slice_fusion.1
  173.2 1.3 constant_dynamic-update-slice_fusion
  174.5 8.7 %constant_dynamic-slice_fusion = bf16[256,14336]{1,0:T(8,128)(2,1)} fusion(bf16[256,28672]{1,0:T(8,128)(2,1)} %constant_dynamic-update-slice_fusion, s32[]{:T(128)S(6)} %select_n.14), kind=kLoop, calls=%fused_computation.21 | loop fusion | bytes 14680068 | tf_op jit(solution)/shard_map/jit(_roll_dynamic)/dynamic_slice | solution.py:15
  183.2 10.4 %copy.6 = bf16[256,14336]{0,1:T(8,128)(2,1)} copy(bf16[256,14336]{1,0:T(8,128)(2,1)} %constant_dynamic-slice_fusion) | data formatting | bytes 14680064 | tf_op jit(solution)/shard_map/jit(_roll_dynamic)/dynamic_slice | solution.py:15
  193.6 88.3 %all_to_all.19 = bf16[256,8,1792]{0,2,1:T(8,128)(2,1)} all-to-all(bf16[256,8,1792]{0,2,1:T(8,128)(2,1)} %bitcast.7), channel_id=1, replica_groups=mesh['dp'=8,'tensor'=4] {'dp'}, dimensions={1} | all-to-all | bytes 14680064 | tf_op jit(solution)/shard_map/all_to_all | solution.py:30
  282.0 10.1 %copy.7 = bf16[8,256,1792]{2,1,0:T(8,128)(2,1)} copy(bf16[8,256,1792]{1,2,0:T(8,128)(2,1)} %bitcast.8) | data formatting | bytes 14680064 | tf_op jit(solution)/shard_map/all_to_all | solution.py:30
  292.0 0.0 all-gather.2.cloned.1.call-done
  292.0 0.0 copy-start.1
  292.0 33.9 %convolution_multiply_fusion = f32[1792,3584]{1,0:T(8,128)} fusion(bf16[2048,1792]{1,0:T(8,128)(2,1)} %bitcast.9, bf16[2048,3584]{1,0:T(8,128)(2,1)} %all-gather.2.cloned.1.call-done), kind=kOutput, calls=%fused_computation | convolution fusion | flops 26313097216 | bytes 47710208 | tf_op jit(solution)/shard_map/dot_general | solution.py:31
  325.9 0.0 copy-done.1
Async XLA Ops:
  7.2 1.6 copy-start
  7.2 284.9 %all-gather.2.cloned.1.call-start = ((), (), s32[]{:S(2)}) async-start(), calls=%async_computation.1 | async-start | bytes 16515072 | tf_op jit(solution)/shard_map/all_gather | solution.py:33
  25.6 139.2 %copy-start.2 = (bf16[256,3584]{1,0:T(8,128)(2,1)S(1)}, bf16[256,3584]{1,0:T(8,128)(2,1)}, u32[]{:S(2)}) copy-start(bf16[256,3584]{1,0:T(8,128)(2,1)} %get-tuple-element.3) | copy-start | bytes 5505028
  25.7 45.3 %collective-permute-start = (bf16[256,3584]{1,0:T(8,128)(2,1)}, bf16[256,3584]{1,0:T(8,128)(2,1)S(1)}, u32[]{:S(2)}, u32[]{:S(2)}) collective-permute-start(bf16[256,3584]{1,0:T(8,128)(2,1)} %get-tuple-element.3), channel_id=1, source_target_pairs={{0,1},{1,2},{2,3},{3,0},{4,5},{5,6},{6,7},{7,4},{8,9},{9,10},{10,1... | collective-permute-start | bytes 5505032 | tf_op jit(solution)/shard_map/ppermute | solution.py:12
  71.0 1.2 copy-start.3
  72.3 43.1 %collective-permute-start.1 = (bf16[256,3584]{1,0:T(8,128)(2,1)S(1)}, bf16[256,3584]{1,0:T(8,128)(2,1)}, u32[]{:S(2)}, u32[]{:S(2)}) collective-permute-start(bf16[256,3584]{1,0:T(8,128)(2,1)S(1)} %collective-permute-done), channel_id=1, source_target_pairs={{0,1},{1,2},{2,3},{3,0},{4,5},{5,6},{6,7},{7,4},{8,9},{9,10},{10,1... | collective-permute-start | bytes 5505032 | tf_op jit(solution)/shard_map/ppermute | solution.py:12
  115.3 42.4 %collective-permute-start.2 = (bf16[256,3584]{1,0:T(8,128)(2,1)}, bf16[256,3584]{1,0:T(8,128)(2,1)}, u32[]{:S(2)}, u32[]{:S(2)}) collective-permute-start(bf16[256,3584]{1,0:T(8,128)(2,1)} %collective-permute-done.1), channel_id=1, source_target_pairs={{0,1},{1,2},{2,3},{3,0},{4,5},{5,6},{6,7},{7,4},{8,9},{9,10},{10,1... | collective-permute-start | bytes 5505032 | tf_op jit(solution)/shard_map/ppermute | solution.py:12
  115.3 48.1 %copy-start.4 = (bf16[256,3584]{1,0:T(8,128)(2,1)S(1)}, bf16[256,3584]{1,0:T(8,128)(2,1)}, u32[]{:S(2)}) copy-start(bf16[256,3584]{1,0:T(8,128)(2,1)} %copy-done.3) | copy-start | bytes 5505028
  292.0 33.9 %copy-start.1 = (bf16[256,4096]{1,0:T(8,128)(2,1)S(1)}, bf16[256,4096]{1,0:T(8,128)(2,1)}, u32[]{:S(2)}) copy-start(bf16[256,4096]{1,0:T(8,128)(2,1)} %param.4) | copy-start | bytes 6291460
Sparse Core Ops, SparseCore 0:
  25.8 83.5 all-gather.1
